TPU v7x, 32 devices: a whole 2x2x4 slice. The times are simulated.
32 devices in a mesh: smp: 8 (over z, y), var: 4 (over x, core).
Axes of the slice: x: 2, y: 2, z: 4, core: 2. Of those that a mesh axis runs over, the one named last changes fastest.
Arguments:
- dosage: int32 [512, 2048], P('smp', 'var'), may hold values from -2147483648 to 2147483647, as said below
- shares_init: float32 [12, 8192], P(None, ('smp', 'var')), may hold values from 0.1 to 1
- freqs_init: float32 [12, 2048], P(None, ('var', 'smp')), may hold values from 0.019 to 0.981
Outputs:
- shares: float32 [12, 8192], P(None, ('smp', 'var'))
- freqs: float32 [12, 2048], P(None, ('var', 'smp'))
Inputs may be any that keep to these rules, and one draw needn't show every extreme that they name: Every 2-bit code in a word of dosage is 0, 1, 2 or 3, and 3 marks a missing genotype.
All inputs are finite; a program needn't handle non-finite values.
Results may differ from a plain program's by a relative error of at most 0.0003.
Values sent between devices are 32-bit elements; how exact they have to be, the bound alone decides.
A program may use at most 64 MiB of HBM per device.

v0:
```python
import functools

import jax
import jax.numpy as jnp
from jax import lax
from jax.experimental import pallas as pl
from jax.experimental.pallas import tpu as pltpu
from jax.sharding import PartitionSpec as P

ITERS = 2
CODES = 16
PAD = 16
F32 = jnp.float32
BF16 = jnp.bfloat16


def split(x, pieces):
    out = []
    for _ in range(pieces):
        piece = x.astype(BF16)
        out.append(piece)
        x = x - piece.astype(F32)
    return out


def dot(a, b):
    return jnp.dot(a, b, preferred_element_type=F32)


def dot_nt(a, b):
    return lax.dot_general(a, b, (((1,), (1,)), ((), ())), preferred_element_type=F32)


def em_kernel(
    nv, ns, chunk, dosage_hbm, shares_hbm, freqs_hbm, shares_out, freqs_out,
    dosage_ref, shares_ref, freqs_ref, q_slots, f_slots, sq_send, sq_recv, sf_send, sf_recv,
    q_pad, f_pad, qt_ref, q2_ref, fs_ref, fgs_ref,
    load_sem, q_ss, q_rs, f_ss, f_rs, sq_ss, sq_rs, sf_ss, sf_rs,
):
    iv, js = lax.axis_index("var"), lax.axis_index("smp")
    pops, ws = shares_ref.shape
    wf = freqs_ref.shape[1]
    words, variants = dosage_ref.shape
    samples = words * CODES
    chunks = variants // chunk
    per = ns // chunks
    own_chunk, own_place = js // per, lax.rem(js, per)
    mesh_ids = pl.DeviceIdType.MESH

    def chunk_at(t):
        return lax.rem(own_chunk + t, chunks)

    def smp_peer(t, d):
        return chunk_at(t) * per + lax.rem(own_place + d, per)

    def var_peer(d):
        return lax.rem(iv + d, nv)

    smp_peers = [[smp_peer(t, d) for d in range(0 if t else 1, per)] for t in range(chunks)]
    all_smp = [p for t in reversed(range(chunks)) for p in smp_peers[t]]
    var_peers = [var_peer(d) for d in range(1, nv)]

    barrier = pltpu.get_barrier_semaphore()
    for p in all_smp:
        pl.semaphore_signal(barrier, inc=1, device_id=(p, iv), device_id_type=mesh_ids)
    for p in var_peers:
        pl.semaphore_signal(barrier, inc=1, device_id=(js, p), device_id_type=mesh_ids)

    load_q = pltpu.make_async_copy(shares_hbm, shares_ref, load_sem.at[0])
    load_f = pltpu.make_async_copy(freqs_hbm, f_slots.at[0, js], load_sem.at[1])
    load_f2 = pltpu.make_async_copy(freqs_hbm, freqs_ref, load_sem.at[2])
    load_d = pltpu.make_async_copy(dosage_hbm, dosage_ref, load_sem.at[3])
    load_q.start()
    load_f.start()
    load_f2.start()
    load_d.start()
    q_pad[...] = jnp.zeros_like(q_pad)
    f_pad[...] = jnp.zeros_like(f_pad)
    load_q.wait()
    q_own = shares_ref[...]
    q_own = q_own / jnp.sum(q_own, axis=0, keepdims=True)
    q_slots[0, iv] = q_own
    load_f.wait()
    load_f2.wait()
    f_own = freqs_ref[...]
    pl.semaphore_wait(barrier, ns - 1 + nv - 1)

    def smp_copy(src, dst, it, ss, rs, to, slot):
        return pltpu.make_async_remote_copy(
            src_ref=src, dst_ref=dst.at[it, slot], send_sem=ss.at[it, to], recv_sem=rs.at[it, slot],
            device_id=(to, iv), device_id_type=mesh_ids)

    def var_copy(src, dst, it, ss, rs, to, slot):
        return pltpu.make_async_remote_copy(
            src_ref=src, dst_ref=dst.at[it, slot], send_sem=ss.at[it, to], recv_sem=rs.at[it, slot],
            device_id=(js, to), device_id_type=mesh_ids)

    sent = []

    def start(copy):
        copy.start()
        sent.append(copy)

    rows = 512
    blocks = samples // rows
    for it in range(ITERS):
        last = it + 1 == ITERS
        if it == 0:
            for p in all_smp:
                start(smp_copy(f_slots.at[it, js], f_slots, it, f_ss, f_rs, p, js))
            for p in var_peers:
                start(var_copy(q_slots.at[it, iv], q_slots, it, q_ss, q_rs, p, iv))

        for p in var_peers:
            var_copy(q_slots.at[it, iv], q_slots, it, q_ss, q_rs, p, p).wait_recv()
        for v in range(nv):
            q_pad[0:pops, v * ws:(v + 1) * ws] = q_slots[it, v]
        qh, qm, ql = split(q_pad[...], 3)
        qs = jnp.concatenate([qh, qh, qm, qh, qm, ql, qm, ql], axis=0)
        qt_ref[...] = qs.astype(F32).T.astype(BF16)
        q2_ref[...] = jnp.concatenate([qh, qm], axis=0)
        if it == 0:
            load_d.wait()

        sq_acc = [jnp.zeros((2 * PAD, rows), F32) for _ in range(blocks)]
        for t in range(chunks):
            c = chunk_at(t)
            for p in smp_peers[t]:
                smp_copy(f_slots.at[it, js], f_slots, it, f_ss, f_rs, p, p).wait_recv()
            for i in range(per):
                f_pad[0:pops, i * wf:(i + 1) * wf] = f_slots[it, c * per + i]
            f_all = f_pad[...]
            fh, fm, fl = split(f_all, 3)
            gh, gm = split(1.0 - f_all, 2)
            fs_ref[...] = jnp.concatenate([fh, fm, fh, fl, fm, fh, fl, fm], axis=0)
            fpair = jnp.concatenate([fh, fm], axis=0)
            gpair = jnp.concatenate([gh, gm], axis=0)
            fgs_ref[...] = jnp.concatenate([fpair, fpair, gpair, gpair], axis=1)

            kept = []
            sum_a = jnp.zeros((2 * PAD, chunk), F32)
            sum_b = jnp.zeros((2 * PAD, chunk), F32)
            lanes = pl.ds(pl.multiple_of(c * chunk, chunk), chunk)
            for b in range(blocks):
                here = slice(b * rows, (b + 1) * rows)
                packed = dosage_ref[b * rows // CODES:(b + 1) * rows // CODES, lanes]
                shape3 = (rows // CODES, CODES, chunk)
                shifts = 2 * lax.broadcasted_iota(jnp.int32, shape3, 1)
                codes = jnp.bitwise_and(jnp.right_shift(jnp.broadcast_to(packed[:, None, :], shape3), shifts), 3)
                codes = codes.reshape(rows, chunk)
                probs = dot(qt_ref[here, :], fs_ref[...])
                rest = 1.0 - probs
                inv = 1.0 / (probs * rest)
                live = codes < 3
                codes_f = codes.astype(F32)
                a = jnp.where(live, codes_f, 0.0) * (rest * inv)
                bb = jnp.where(live, 2.0 - codes_f, 0.0) * (probs * inv)
                ah, al = split(a, 2)
                bh, bl = split(bb, 2)
                q2 = q2_ref[:, here]
                q22 = jnp.concatenate([q2, q2], axis=1)
                sum_a = sum_a + dot(q22, jnp.concatenate([ah, al], axis=0))
                sum_b = sum_b + dot(q22, jnp.concatenate([bh, bl], axis=0))
                kept.append(jnp.concatenate([ah, al, bh, bl], axis=1))
                if t + 1 < chunks:
                    sq_acc[b] = sq_acc[b] + dot_nt(fgs_ref[...], kept[b])
            sum_a = (sum_a[0:PAD] + sum_a[PAD:2 * PAD])[0:pops]
            sum_b = (sum_b[0:PAD] + sum_b[PAD:2 * PAD])[0:pops]
            for i in range(per):
                cut = slice(i * wf, (i + 1) * wf)
                sf_send[it, c * per + i] = jnp.concatenate([sum_a[:, cut], sum_b[:, cut]], axis=1)
            for p in smp_peers[t]:
                start(smp_copy(sf_send.at[it, p], sf_recv, it, sf_ss, sf_rs, p, js))

        for b in range(blocks):
            sq_acc[b] = sq_acc[b] + dot_nt(fgs_ref[...], kept[b])
        sum_q = jnp.concatenate([x[0:PAD] + x[PAD:2 * PAD] for x in sq_acc], axis=1)[0:pops]
        for v in range(nv):
            sq_send[it, v] = sum_q[:, v * ws:(v + 1) * ws]
        for p in var_peers:
            start(var_copy(sq_send.at[it, p], sq_recv, it, sq_ss, sq_rs, p, iv))

        total = sq_send[it, iv]
        for p in var_peers:
            var_copy(sq_send.at[it, p], sq_recv, it, sq_ss, sq_rs, p, p).wait_recv()
            total = total + sq_recv[it, p]
        numer = q_own * total
        q_own = (numer + 0.5) / (jnp.sum(numer, axis=0, keepdims=True) + 0.5 * pops)
        if last:
            shares_out[...] = q_own
        else:
            q_slots[it + 1, iv] = q_own
            for p in var_peers:
                start(var_copy(q_slots.at[it + 1, iv], q_slots, it + 1, q_ss, q_rs, p, iv))

        total = sf_send[it, js]
        for t in range(chunks):
            for p in smp_peers[t]:
                smp_copy(sf_send.at[it, p], sf_recv, it, sf_ss, sf_rs, p, p).wait_recv()
                total = total + sf_recv[it, p]
        alt_part = f_own * total[:, 0:wf]
        ref_part = (1.0 - f_own) * total[:, wf:2 * wf]
        f_own = (alt_part + 0.5) / (alt_part + ref_part + 1.0)
        if last:
            freqs_out[...] = f_own
        else:
            f_slots[it + 1, js] = f_own
            for p in all_smp:
                start(smp_copy(f_slots.at[it + 1, js], f_slots, it + 1, f_ss, f_rs, p, js))

    for copy in sent:
        copy.wait_send()


def hand_out(shares_ref, freqs_ref, shares_out, freqs_out):
    shares_out[...] = shares_ref[...]
    freqs_out[...] = freqs_ref[...]


def body(nv, ns, dosage, shares_init, freqs_init):
    pops, ws = shares_init.shape
    wf = freqs_init.shape[1]
    words, variants = dosage.shape
    samples = words * CODES
    chunk = variants // 2
    vmem = pl.BlockSpec(memory_space=pltpu.VMEM)
    hbm = pl.BlockSpec(memory_space=pl.ANY)
    dma = pltpu.SemaphoreType.DMA
    shapes = (jax.ShapeDtypeStruct((pops, ws), F32), jax.ShapeDtypeStruct((pops, wf), F32))
    shares, freqs = pl.pallas_call(
        functools.partial(em_kernel, nv, ns, chunk),
        out_shape=shapes,
        in_specs=[hbm, hbm, hbm],
        out_specs=(vmem, vmem),
        scratch_shapes=[
            pltpu.VMEM((words, variants), jnp.int32),
            pltpu.VMEM((pops, ws), F32),
            pltpu.VMEM((pops, wf), F32),
            pltpu.VMEM((ITERS, nv, pops, ws), F32),
            pltpu.VMEM((ITERS, ns, pops, wf), F32),
            pltpu.VMEM((ITERS, nv, pops, ws), F32),
            pltpu.VMEM((ITERS, nv, pops, ws), F32),
            pltpu.VMEM((ITERS, ns, pops, 2 * wf), F32),
            pltpu.VMEM((ITERS, ns, pops, 2 * wf), F32),
            pltpu.VMEM((PAD, samples), F32),
            pltpu.VMEM((PAD, chunk), F32),
            pltpu.VMEM((samples, 8 * PAD), BF16),
            pltpu.VMEM((2 * PAD, samples), BF16),
            pltpu.VMEM((8 * PAD, chunk), BF16),
            pltpu.VMEM((2 * PAD, 4 * chunk), BF16),
            dma((4,)),
            dma((ITERS, nv)), dma((ITERS, nv)),
            dma((ITERS, ns)), dma((ITERS, ns)),
            dma((ITERS, nv)), dma((ITERS, nv)),
            dma((ITERS, ns)), dma((ITERS, ns)),
        ],
        compiler_params=pltpu.CompilerParams(collective_id=0, has_side_effects=True),
        cost_estimate=pl.CostEstimate(flops=200000000, bytes_accessed=400000, transcendentals=1000000),
    )(dosage, shares_init, freqs_init)
    return pl.pallas_call(
        hand_out, out_shape=shapes, in_specs=[vmem, vmem], out_specs=(vmem, vmem),
    )(shares, freqs)


def solution(mesh):
    placed = (P("smp", "var"), P(None, ("smp", "var")), P(None, ("var", "smp")))
    return jax.shard_map(
        functools.partial(body, mesh.shape["var"], mesh.shape["smp"]),
        mesh=mesh,
        in_specs=placed,
        out_specs=(P(None, ("smp", "var")), P(None, ("var", "smp"))),
        check_vma=False,
    )
```

profile of v0, /device:TPU:0, one launch (start us, length us, event | category | flops | bytes accessed | tf_op | source)
XLA Modules:
  0.0 29.9 jit_solution(3038262798914331974)
XLA Ops:
  0.6 28.0 %shard_map.50 = (f32[12,256]{1,0:T(8,128)}, f32[12,64]{1,0:T(8,128)}) custom-call(s32[64,512]{1,0:T(8,128)} %dosage_hbm.1, f32[12,256]{1,0:T(8,128)} %shares_hbm.1, f32[12,64]{1,0:T(8,128)} %freqs_hbm.1), custom_call_target="tpu_custom_call" | custom-call | flops 200000000 | bytes 400000 | tf_op jit(solution)/shard_map/pallas_call | solution.py:230
  28.6 1.3 %shard_map.51 = (f32[12,256]{1,0:T(8,128)}, f32[12,64]{1,0:T(8,128)}) custom-call(f32[12,256]{1,0:T(8,128)} %get-tuple-element.4.shares_ref, f32[12,64]{1,0:T(8,128)} %get-tuple-element.5.freqs_ref), custom_call_target="tpu_custom_call" | custom-call | tf_op jit(solution)/shard_map/pallas_call | solution.py:260
where the time goes:
time: 30.3 us; the launch traced here: 29.9 us
  Pallas kernels  29.3 us (97%)
  between operations  0.64 us (2%)
    pallas_call x1, Pallas kernels, body(): pl.pallas_call(functools.partial(em_kernel, nv, ns, chunk), out_shape=sha...  28 us
    pallas_call x1, Pallas kernels, body(): pl.pallas_call(hand_out, out_shape=shapes, in_specs=[vmem, vmem], out_spe...  1.33 us

commit v1 on v0

v1 whole, which is shorter than its diff:
```python
import functools

import jax
import jax.numpy as jnp
from jax import lax
from jax.experimental import pallas as pl
from jax.experimental.pallas import tpu as pltpu
from jax.sharding import PartitionSpec as P

ITERS = 2
CODES = 16
PAD = 16
ROWS = 512
F32 = jnp.float32
BF16 = jnp.bfloat16


def split(x, pieces):
    out = []
    for _ in range(pieces):
        piece = x.astype(BF16)
        out.append(piece)
        x = x - piece.astype(F32)
    return out


def dot(a, b):
    return jnp.dot(a, b, preferred_element_type=F32)


def dot_nt(a, b):
    return lax.dot_general(a, b, (((1,), (1,)), ((), ())), preferred_element_type=F32)


def em_kernel(
    nv, ns, dosage_hbm, shares_hbm, freqs_hbm, shares_out, freqs_out,
    dosage_ref, shares_ref, freqs_ref, alt_ref, ref_ref,
    q_slots, f_slots, c_slots, sq_send, sq_recv, sc_send, sc_recv, sf_send, sf_recv,
    q_pad, f_pad, qt_ref, qd_ref, qb_ref, fs_ref, fgs_ref,
    load_sem, q_ss, q_rs, f_ss, f_rs, c_ss, c_rs, sq_ss, sq_rs, sc_ss, sc_rs, sf_ss, sf_rs,
):
    iv, js = lax.axis_index("var"), lax.axis_index("smp")
    pops, ws = shares_ref.shape
    wf = freqs_ref.shape[1]
    words, variants = dosage_ref.shape
    samples = words * CODES
    half = ns // 2
    mids = half // 2
    chunk = variants // 2
    wc = chunk // mids
    side = js // half
    mesh_ids = pl.DeviceIdType.MESH

    def other_smp(d):
        return lax.rem(js + d, ns)

    def middle(c, i):
        return (1 - c) * half + c * (half - mids) + i

    my_mid_chunk = 1 - side
    my_mid = js - middle(my_mid_chunk, 0)
    is_mid = jnp.logical_and(js >= half - mids, js < half + mids)
    smp_peers = [other_smp(d) for d in range(1, ns)]
    var_peers = [lax.rem(iv + d, nv) for d in range(1, nv)]

    barrier = pltpu.get_barrier_semaphore()
    for p in smp_peers:
        pl.semaphore_signal(barrier, inc=1, device_id=(p, iv), device_id_type=mesh_ids)
    for p in var_peers:
        pl.semaphore_signal(barrier, inc=1, device_id=(js, p), device_id_type=mesh_ids)

    load_q = pltpu.make_async_copy(shares_hbm, shares_ref, load_sem.at[0])
    load_f = pltpu.make_async_copy(freqs_hbm, f_slots.at[js], load_sem.at[1])
    load_d = pltpu.make_async_copy(dosage_hbm, dosage_ref, load_sem.at[2])
    load_q.start()
    load_f.start()
    load_d.start()
    q_pad[...] = jnp.zeros_like(q_pad)
    f_pad[...] = jnp.zeros_like(f_pad)
    load_q.wait()
    q_own = shares_ref[...]
    q_own = q_own / jnp.sum(q_own, axis=0, keepdims=True)
    q_slots[0, iv] = q_own
    load_f.wait()
    pl.semaphore_wait(barrier, ns - 1 + nv - 1)

    def smp_copy(src, dst, ss, rs, to):
        return pltpu.make_async_remote_copy(
            src_ref=src, dst_ref=dst, send_sem=ss, recv_sem=rs, device_id=(to, iv), device_id_type=mesh_ids)

    def var_copy(src, dst, ss, rs, to):
        return pltpu.make_async_remote_copy(
            src_ref=src, dst_ref=dst, send_sem=ss, recv_sem=rs, device_id=(js, to), device_id_type=mesh_ids)

    def f_copy(to, slot):
        return smp_copy(f_slots.at[slot], f_slots.at[slot], f_ss.at[to], f_rs.at[slot], to)

    def q_copy(it, to, slot):
        return var_copy(q_slots.at[it, slot], q_slots.at[it, slot], q_ss.at[it, to], q_rs.at[it, slot], to)

    def sq_copy(it, to, slot):
        return var_copy(sq_send.at[it, to], sq_recv.at[it, slot], sq_ss.at[it, to], sq_rs.at[it, slot], to)

    def sf_copy(to, slot):
        return smp_copy(sf_send.at[to], sf_recv.at[slot], sf_ss.at[to], sf_rs.at[slot], to)

    def sc_copy(it, c, i, to, slot):
        return smp_copy(sc_send.at[it, c, i], sc_recv.at[it, slot], sc_ss.at[it, c, i], sc_rs.at[it, slot], to)

    def c_copy(it, to, slot):
        return smp_copy(c_slots.at[it, slot], c_slots.at[it, slot], c_ss.at[it, to], c_rs.at[it, slot], to)

    sent = []

    def start(copy, when=None):
        sent.append((copy, when))
        if when is None:
            copy.start()
        else:
            pl.when(when)(copy.start)

    for p in smp_peers:
        start(f_copy(p, js))
    for p in var_peers:
        start(q_copy(0, p, iv))

    load_d.wait()
    blocks = samples // ROWS
    ones = jnp.ones((8, chunk), BF16)
    counts = []
    for b in range(blocks):
        here = slice(b * ROWS, (b + 1) * ROWS)
        count = jnp.zeros((8, ROWS), F32)
        for c in range(2):
            packed = dosage_ref[b * ROWS // CODES:(b + 1) * ROWS // CODES, c * chunk:(c + 1) * chunk]
            shape3 = (ROWS // CODES, CODES, chunk)
            shifts = 2 * lax.broadcasted_iota(jnp.int32, shape3, 1)
            codes = jnp.bitwise_and(jnp.right_shift(jnp.broadcast_to(packed[:, None, :], shape3), shifts), 3)
            codes = codes.reshape(ROWS, chunk)
            live = codes < 3
            alt = jnp.where(live, codes.astype(F32), 0.0)
            both = jnp.where(live, 2.0, 0.0)
            alt_ref[c, here, :] = alt
            ref_ref[c, here, :] = both - alt
            count = count + dot_nt(ones, both.astype(BF16))
        counts.append(count[0:1])
    counts = jnp.concatenate(counts, axis=1)

    for it in range(ITERS):
        last = it + 1 == ITERS

        for p in var_peers:
            q_copy(it, p, p).wait_recv()
        for v in range(nv):
            q_pad[0:pops, v * ws:(v + 1) * ws] = q_slots[it, v]
        qh, qm, ql = split(q_pad[...], 3)
        qs = jnp.concatenate([qh, qh, qm, qh, qm, ql, qm, ql], axis=0)
        qt_ref[...] = qs.astype(F32).T.astype(BF16)
        none = jnp.zeros_like(qh)
        qd_ref[...] = jnp.concatenate([qh, none, qm, none], axis=0)
        qb_ref[...] = jnp.concatenate([none, qh, none, qm], axis=0)

        sq_acc = [jnp.zeros((2 * PAD, ROWS), F32) for _ in range(blocks)]
        for t in range(2):
            c = side if (it == 0) == (t == 0) else 1 - side
            if it == 0:
                for i in range(half):
                    p = c * half + lax.rem(js + i, half)
                    if t or i:
                        f_copy(p, p).wait_recv()
                for i in range(half):
                    f_pad[0:pops, i * wf:(i + 1) * wf] = f_slots[c * half + i]
            else:
                for i in range(mids):
                    slot = c * mids + i
                    copy = c_copy(it, js, slot)
                    pl.when(middle(c, i) != js)(copy.wait_recv)
                for i in range(mids):
                    f_pad[0:pops, i * wc:(i + 1) * wc] = c_slots[it, c * mids + i]
            f_all = f_pad[...]
            fh, fm, fl = split(f_all, 3)
            fs_ref[...] = jnp.concatenate([fh, fm, fh, fl, fm, fh, fl, fm], axis=0)
            fpair = jnp.concatenate([fh, fm], axis=0)
            fgs_ref[...] = jnp.concatenate([fpair, fpair], axis=1)

            kept = []
            sums = jnp.zeros((4 * PAD, chunk), F32)
            for b in range(blocks):
                here = slice(b * ROWS, (b + 1) * ROWS)
                probs = dot(qt_ref[here, :], fs_ref[...])
                rest = 1.0 - probs
                inv = 1.0 / (probs * rest)
                alt = alt_ref[c, here, :] * rest
                bb = ref_ref[c, here, :] * probs
                dd = (alt - bb) * inv
                bb = bb * inv
                dh, dl = split(dd, 2)
                bh, bl = split(bb, 2)
                qd, qb = qd_ref[:, here], qb_ref[:, here]
                sums = sums + dot(
                    jnp.concatenate([qd, qd, qb, qb], axis=1), jnp.concatenate([dh, dl, bh, bl], axis=0))
                kept.append(jnp.concatenate([dh, dl], axis=1))
                if t == 0:
                    sq_acc[b] = sq_acc[b] + dot_nt(fgs_ref[...], kept[b])
            sums = sums[0:2 * PAD] + sums[2 * PAD:4 * PAD]
            sum_d, sum_b = sums[0:pops], sums[PAD:PAD + pops]
            if last:
                for i in range(half):
                    cut = slice(i * wf, (i + 1) * wf)
                    sf_send[c * half + i] = jnp.concatenate([sum_d[:, cut], sum_b[:, cut]], axis=1)
                for i in range(half):
                    p = c * half + lax.rem(js + i, half)
                    if i or t == 0:
                        start(sf_copy(p, js))
            else:
                stacked = jnp.concatenate([sum_d, sum_b], axis=0)
                for i in range(mids):
                    sc_send[it, c, i] = stacked[:, i * wc:(i + 1) * wc]
                for i in range(mids):
                    to = middle(c, i)
                    start(sc_copy(it, c, i, to, js), to != js)

        for b in range(blocks):
            sq_acc[b] = sq_acc[b] + dot_nt(fgs_ref[...], kept[b])
        sum_q = jnp.concatenate([x[0:PAD] + x[PAD:2 * PAD] for x in sq_acc], axis=1)
        sum_q = sum_q + (counts - jnp.sum(q_pad[...] * sum_q, axis=0, keepdims=True))
        sum_q = sum_q[0:pops]
        for v in range(nv):
            sq_send[it, v] = sum_q[:, v * ws:(v + 1) * ws]
        for p in var_peers:
            start(sq_copy(it, p, iv))

        total = sq_send[it, iv]
        for p in var_peers:
            sq_copy(it, p, p).wait_recv()
            total = total + sq_recv[it, p]
        numer = q_own * total
        q_own = (numer + 0.5) / (jnp.sum(numer, axis=0, keepdims=True) + 0.5 * pops)
        if last:
            shares_out[...] = q_own
        else:
            q_slots[it + 1, iv] = q_own
            for p in var_peers:
                start(q_copy(it + 1, p, iv))

        if last:
            place = lax.rem(js, half)
            pair = c_slots[it, side * mids + place // 2]
            f_own = jnp.where(lax.rem(place, 2) == 0, pair[:, 0:wf], pair[:, wf:2 * wf])
            total = sf_send[js]
            for p in smp_peers:
                sf_copy(p, p).wait_recv()
                total = total + sf_recv[p]
            sum_d, sum_b = total[:, 0:wf], total[:, wf:2 * wf]
            freqs_out[...] = (f_own * (sum_d + sum_b) + 0.5) / (f_own * sum_d + sum_b + 1.0)
        else:
            slot = my_mid_chunk * mids + my_mid

            @pl.when(is_mid)
            def _():
                total = sc_send[it, my_mid_chunk, my_mid]
                for p in smp_peers:
                    sc_copy(it, my_mid_chunk, my_mid, js, p).wait_recv()
                    total = total + sc_recv[it, p]
                if it == 0:
                    first = my_mid_chunk * half + 2 * my_mid
                    f_old = jnp.concatenate([f_slots[first], f_slots[first + 1]], axis=1)
                else:
                    f_old = c_slots[it, slot]
                sum_d, sum_b = total[0:pops], total[pops:2 * pops]
                c_slots[it + 1, slot] = (f_old * (sum_d + sum_b) + 0.5) / (f_old * sum_d + sum_b + 1.0)

            for p in smp_peers:
                start(c_copy(it + 1, p, slot), is_mid)

    for copy, when in sent:
        if when is None:
            copy.wait_send()
        else:
            pl.when(when)(copy.wait_send)


def hand_out(shares_ref, freqs_ref, shares_out, freqs_out):
    shares_out[...] = shares_ref[...]
    freqs_out[...] = freqs_ref[...]


def body(nv, ns, dosage, shares_init, freqs_init):
    pops, ws = shares_init.shape
    wf = freqs_init.shape[1]
    words, variants = dosage.shape
    samples = words * CODES
    chunk = variants // 2
    mids = ns // 4
    wc = chunk // mids
    vmem = pl.BlockSpec(memory_space=pltpu.VMEM)
    hbm = pl.BlockSpec(memory_space=pl.ANY)
    dma = pltpu.SemaphoreType.DMA
    shapes = (jax.ShapeDtypeStruct((pops, ws), F32), jax.ShapeDtypeStruct((pops, wf), F32))
    shares, freqs = pl.pallas_call(
        functools.partial(em_kernel, nv, ns),
        out_shape=shapes,
        in_specs=[hbm, hbm, hbm],
        out_specs=(vmem, vmem),
        scratch_shapes=[
            pltpu.VMEM((words, variants), jnp.int32),
            pltpu.VMEM((pops, ws), F32),
            pltpu.VMEM((pops, wf), F32),
            pltpu.VMEM((2, samples, chunk), F32),
            pltpu.VMEM((2, samples, chunk), F32),
            pltpu.VMEM((ITERS, nv, pops, ws), F32),
            pltpu.VMEM((ns, pops, wf), F32),
            pltpu.VMEM((ITERS, 2 * mids, pops, wc), F32),
            pltpu.VMEM((ITERS, nv, pops, ws), F32),
            pltpu.VMEM((ITERS, nv, pops, ws), F32),
            pltpu.VMEM((ITERS, 2, mids, 2 * pops, wc), F32),
            pltpu.VMEM((ITERS, ns, 2 * pops, wc), F32),
            pltpu.VMEM((ns, pops, 2 * wf), F32),
            pltpu.VMEM((ns, pops, 2 * wf), F32),
            pltpu.VMEM((PAD, samples), F32),
            pltpu.VMEM((PAD, chunk), F32),
            pltpu.VMEM((samples, 8 * PAD), BF16),
            pltpu.VMEM((4 * PAD, samples), BF16),
            pltpu.VMEM((4 * PAD, samples), BF16),
            pltpu.VMEM((8 * PAD, chunk), BF16),
            pltpu.VMEM((2 * PAD, 2 * chunk), BF16),
            dma((3,)),
            dma((ITERS, nv)), dma((ITERS, nv)),
            dma((ns,)), dma((ns,)),
            dma((ITERS, ns)), dma((ITERS, 2 * mids)),
            dma((ITERS, nv)), dma((ITERS, nv)),
            dma((ITERS, 2, mids)), dma((ITERS, ns)),
            dma((ns,)), dma((ns,)),
        ],
        compiler_params=pltpu.CompilerParams(collective_id=0, has_side_effects=True),
        cost_estimate=pl.CostEstimate(flops=200000000, bytes_accessed=400000, transcendentals=1000000),
    )(dosage, shares_init, freqs_init)
    return pl.pallas_call(
        hand_out, out_shape=shapes, in_specs=[vmem, vmem], out_specs=(vmem, vmem),
    )(shares, freqs)


def solution(mesh):
    placed = (P("smp", "var"), P(None, ("smp", "var")), P(None, ("var", "smp")))
    return jax.shard_map(
        functools.partial(body, mesh.shape["var"], mesh.shape["smp"]),
        mesh=mesh,
        in_specs=placed,
        out_specs=(P(None, ("smp", "var")), P(None, ("var", "smp"))),
        check_vma=False,
    )
```

time: 30.3 us -> 28.3 us (0.934)
  Pallas kernels: 29.3 us -> 27.3 us
    pallas_call x1, Pallas kernels: 28 us -> 25.9 us  [body(): pl.pallas_call(functools.partial(em_kernel, nv, ns), out_shape=shapes, in...]
where the time goes in v1:
time: 28.3 us; the launch traced here: 27.9 us
  Pallas kernels  27.3 us (96%)
  between operations  0.64 us (2%)
    pallas_call x1, Pallas kernels, body(): pl.pallas_call(functools.partial(em_kernel, nv, ns), out_shape=shapes, in...  25.9 us
    pallas_call x1, Pallas kernels, body(): pl.pallas_call(hand_out, out_shape=shapes, in_specs=[vmem, vmem], out_spe...  1.33 us

profile of v1, /device:TPU:0, one launch (start us, length us, event | category | flops | bytes accessed | tf_op | source)
XLA Modules:
  0.0 27.9 jit_solution(9414062594779521412)
XLA Ops:
  0.6 25.9 %shard_map.50 = (f32[12,256]{1,0:T(8,128)}, f32[12,64]{1,0:T(8,128)}) custom-call(s32[64,512]{1,0:T(8,128)} %dosage_hbm.1, f32[12,256]{1,0:T(8,128)} %shares_hbm.1, f32[12,64]{1,0:T(8,128)} %freqs_hbm.1), custom_call_target="tpu_custom_call" | custom-call | flops 200000000 | bytes 400000 | tf_op jit(solution)/shard_map/pallas_call | solution.py:300
  26.6 1.3 %shard_map.51 = (f32[12,256]{1,0:T(8,128)}, f32[12,64]{1,0:T(8,128)}) custom-call(f32[12,256]{1,0:T(8,128)} %get-tuple-element.4.shares_ref, f32[12,64]{1,0:T(8,128)} %get-tuple-element.5.freqs_ref), custom_call_target="tpu_custom_call" | custom-call | tf_op jit(solution)/shard_map/pallas_call | solution.py:338

commit v2 on v1

--- a/solution.py
+++ b/solution.py
@@ -299,7 +299,7 @@
     shapes = (jax.ShapeDtypeStruct((pops, ws), F32), jax.ShapeDtypeStruct((pops, wf), F32))
     shares, freqs = pl.pallas_call(
         functools.partial(em_kernel, nv, ns),
-        out_shape=shapes,
+        out_shape=(pltpu.VMEM((pops, ws), F32), pltpu.VMEM((pops, wf), F32)),
         in_specs=[hbm, hbm, hbm],
         out_specs=(vmem, vmem),
         scratch_shapes=[
@@ -335,6 +335,8 @@
         compiler_params=pltpu.CompilerParams(collective_id=0, has_side_effects=True),
         cost_estimate=pl.CostEstimate(flops=200000000, bytes_accessed=400000, transcendentals=1000000),
     )(dosage, shares_init, freqs_init)
+    shares = pltpu.with_memory_space_constraint(shares, pltpu.VMEM)
+    freqs = pltpu.with_memory_space_constraint(freqs, pltpu.VMEM)
     return pl.pallas_call(
         hand_out, out_shape=shapes, in_specs=[vmem, vmem], out_specs=(vmem, vmem),
     )(shares, freqs)

time: 28.3 us -> 26.8 us (0.947)
  Pallas kernels: 27.3 us -> 26 us
    pallas_call x1, Pallas kernels: 1.33 us -> 0.61 us  [body(): pl.pallas_call(hand_out, out_shape=shapes, in_specs=[vmem, vmem], out_spe...]
    pallas_call x1, Pallas kernels: 25.9 us -> 25.3 us  [body(): pl.pallas_call(functools.partial(em_kernel, nv, ns), out_shape=(pltpu.VME...]
where the time goes in v2:
time: 26.8 us; the launch traced here: 26.6 us
  Pallas kernels  26 us (97%)
  between operations  0.64 us (2%)
    pallas_call x1, Pallas kernels, body(): pl.pallas_call(functools.partial(em_kernel, nv, ns), out_shape=(pltpu.VME...  25.3 us
    pallas_call x1, Pallas kernels, body(): pl.pallas_call(hand_out, out_shape=shapes, in_specs=[vmem, vmem], out_spe...  0.61 us

profile of v2, /device:TPU:0, one launch (start us, length us, event | category | flops | bytes accessed | tf_op | source)
XLA Modules:
  0.0 26.6 jit_solution(10147645603539078706)
XLA Ops:
  0.6 25.3 %shard_map.50 = (f32[12,256]{1,0:T(8,128)S(1)}, f32[12,64]{1,0:T(8,128)S(1)}) custom-call(s32[64,512]{1,0:T(8,128)} %dosage_hbm.1, f32[12,256]{1,0:T(8,128)} %shares_hbm.1, f32[12,64]{1,0:T(8,128)} %freqs_hbm.1), custom_call_target="tpu_custom_call" | custom-call | flops 200000000 | bytes 400000 | tf_op jit(solution)/shard_map/pallas_call | solution.py:300
  26.0 0.6 %shard_map.51 = (f32[12,256]{1,0:T(8,128)}, f32[12,64]{1,0:T(8,128)}) custom-call(f32[12,256]{1,0:T(8,128)S(1)} %get-tuple-element.4.shares_ref, f32[12,64]{1,0:T(8,128)S(1)} %get-tuple-element.5.freqs_ref), custom_call_target="tpu_custom_call" | custom-call | tf_op jit(solution)/shard_map/pallas_call | solution.py:340

commit v3 on v2

--- a/solution.py
+++ b/solution.py
@@ -11,6 +11,7 @@
 CODES = 16
 PAD = 16
 ROWS = 512
+LEVELS = 64
 F32 = jnp.float32
 BF16 = jnp.bfloat16
 
@@ -127,22 +128,24 @@
     load_d.wait()
     blocks = samples // ROWS
     ones = jnp.ones((8, chunk), BF16)
+    shape3 = (ROWS // CODES, CODES, chunk)
+    shifts = 2 * lax.broadcasted_iota(jnp.int32, shape3, 1)
+    level = 16 * lax.broadcasted_iota(jnp.int32, shape3, 0) + lax.broadcasted_iota(jnp.int32, shape3, 1)
+    level = jnp.bitwise_and(19 * level + 27 * lax.broadcasted_iota(jnp.int32, shape3, 2), LEVELS - 1)
+    step = (level.astype(F32) - 0.5 * (LEVELS - 1)) * (2.0 ** -7 / LEVELS) + 1.0
     counts = []
     for b in range(blocks):
         here = slice(b * ROWS, (b + 1) * ROWS)
         count = jnp.zeros((8, ROWS), F32)
         for c in range(2):
             packed = dosage_ref[b * ROWS // CODES:(b + 1) * ROWS // CODES, c * chunk:(c + 1) * chunk]
-            shape3 = (ROWS // CODES, CODES, chunk)
-            shifts = 2 * lax.broadcasted_iota(jnp.int32, shape3, 1)
             codes = jnp.bitwise_and(jnp.right_shift(jnp.broadcast_to(packed[:, None, :], shape3), shifts), 3)
-            codes = codes.reshape(ROWS, chunk)
             live = codes < 3
             alt = jnp.where(live, codes.astype(F32), 0.0)
             both = jnp.where(live, 2.0, 0.0)
-            alt_ref[c, here, :] = alt
-            ref_ref[c, here, :] = both - alt
-            count = count + dot_nt(ones, both.astype(BF16))
+            alt_ref[c, here, :] = (alt * step).reshape(ROWS, chunk)
+            ref_ref[c, here, :] = ((both - alt) * step).reshape(ROWS, chunk)
+            count = count + dot_nt(ones, both.reshape(ROWS, chunk).astype(BF16))
         counts.append(count[0:1])
     counts = jnp.concatenate(counts, axis=1)
 
@@ -153,8 +156,8 @@
             q_copy(it, p, p).wait_recv()
         for v in range(nv):
             q_pad[0:pops, v * ws:(v + 1) * ws] = q_slots[it, v]
-        qh, qm, ql = split(q_pad[...], 3)
-        qs = jnp.concatenate([qh, qh, qm, qh, qm, ql, qm, ql], axis=0)
+        qh, qm = split(q_pad[...], 2)
+        qs = jnp.concatenate([qh, qm, qh, qm], axis=0)
         qt_ref[...] = qs.astype(F32).T.astype(BF16)
         none = jnp.zeros_like(qh)
         qd_ref[...] = jnp.concatenate([qh, none, qm, none], axis=0)
@@ -178,10 +181,9 @@
                 for i in range(mids):
                     f_pad[0:pops, i * wc:(i + 1) * wc] = c_slots[it, c * mids + i]
             f_all = f_pad[...]
-            fh, fm, fl = split(f_all, 3)
-            fs_ref[...] = jnp.concatenate([fh, fm, fh, fl, fm, fh, fl, fm], axis=0)
-            fpair = jnp.concatenate([fh, fm], axis=0)
-            fgs_ref[...] = jnp.concatenate([fpair, fpair], axis=1)
+            fh, fm = split(f_all, 2)
+            fs_ref[...] = jnp.concatenate([fh, fh, fm, fm], axis=0)
+            fgs_ref[...] = jnp.concatenate([fh, fm], axis=0)
 
             kept = []
             sums = jnp.zeros((4 * PAD, chunk), F32)
@@ -194,12 +196,9 @@
                 bb = ref_ref[c, here, :] * probs
                 dd = (alt - bb) * inv
                 bb = bb * inv
-                dh, dl = split(dd, 2)
-                bh, bl = split(bb, 2)
-                qd, qb = qd_ref[:, here], qb_ref[:, here]
-                sums = sums + dot(
-                    jnp.concatenate([qd, qd, qb, qb], axis=1), jnp.concatenate([dh, dl, bh, bl], axis=0))
-                kept.append(jnp.concatenate([dh, dl], axis=1))
+                dh, bh = dd.astype(BF16), bb.astype(BF16)
+                sums = sums + (dot(qd_ref[:, here], dh) + dot(qb_ref[:, here], bh))
+                kept.append(dh)
                 if t == 0:
                     sq_acc[b] = sq_acc[b] + dot_nt(fgs_ref[...], kept[b])
             sums = sums[0:2 * PAD] + sums[2 * PAD:4 * PAD]
@@ -319,11 +318,11 @@
             pltpu.VMEM((ns, pops, 2 * wf), F32),
             pltpu.VMEM((PAD, samples), F32),
             pltpu.VMEM((PAD, chunk), F32),
-            pltpu.VMEM((samples, 8 * PAD), BF16),
+            pltpu.VMEM((samples, 4 * PAD), BF16),
             pltpu.VMEM((4 * PAD, samples), BF16),
             pltpu.VMEM((4 * PAD, samples), BF16),
-            pltpu.VMEM((8 * PAD, chunk), BF16),
-            pltpu.VMEM((2 * PAD, 2 * chunk), BF16),
+            pltpu.VMEM((4 * PAD, chunk), BF16),
+            pltpu.VMEM((2 * PAD, chunk), BF16),
             dma((3,)),
             dma((ITERS, nv)), dma((ITERS, nv)),
             dma((ns,)), dma((ns,)),

time: 26.8 us -> 25 us (0.933)
  Pallas kernels: 26 us -> 24.2 us
    pallas_call x1, Pallas kernels: 25.3 us -> 23.6 us  [body(): pl.pallas_call(functools.partial(em_kernel, nv, ns), out_shape=(pltpu.VME...]
where the time goes in v3:
time: 25 us; the launch traced here: 24.8 us
  Pallas kernels  24.2 us (97%)
  between operations  0.64 us (3%)
    pallas_call x1, Pallas kernels, body(): pl.pallas_call(functools.partial(em_kernel, nv, ns), out_shape=(pltpu.VME...  23.6 us
    pallas_call x1, Pallas kernels, body(): pl.pallas_call(hand_out, out_shape=shapes, in_specs=[vmem, vmem], out_spe...  0.61 us

profile of v3, /device:TPU:0, one launch (start us, length us, event | category | flops | bytes accessed | tf_op | source)
XLA Modules:
  0.0 24.8 jit_solution(11184343907824526205)
XLA Ops:
  0.6 23.6 %shard_map.50 = (f32[12,256]{1,0:T(8,128)S(1)}, f32[12,64]{1,0:T(8,128)S(1)}) custom-call(s32[64,512]{1,0:T(8,128)} %dosage_hbm.1, f32[12,256]{1,0:T(8,128)} %shares_hbm.1, f32[12,64]{1,0:T(8,128)} %freqs_hbm.1), custom_call_target="tpu_custom_call" | custom-call | flops 200000000 | bytes 400000 | tf_op jit(solution)/shard_map/pallas_call | solution.py:299
  24.2 0.6 %shard_map.51 = (f32[12,256]{1,0:T(8,128)}, f32[12,64]{1,0:T(8,128)}) custom-call(f32[12,256]{1,0:T(8,128)S(1)} %get-tuple-element.4.shares_ref, f32[12,64]{1,0:T(8,128)S(1)} %get-tuple-element.5.freqs_ref), custom_call_target="tpu_custom_call" | custom-call | tf_op jit(solution)/shard_map/pallas_call | solution.py:339

commit v4 on v3

--- a/solution.py
+++ b/solution.py
@@ -33,12 +33,23 @@
     return lax.dot_general(a, b, (((1,), (1,)), ((), ())), preferred_element_type=F32)
 
 
+def renewed_shares(old, sums):
+    numer = old * sums
+    return (numer + 0.5) / (jnp.sum(numer, axis=0, keepdims=True) + 0.5 * old.shape[0])
+
+
+def renewed_freqs(old, sum_d, sum_b):
+    return (old * (sum_d + sum_b) + 0.5) / (old * sum_d + sum_b + 1.0)
+
+
 def em_kernel(
     nv, ns, dosage_hbm, shares_hbm, freqs_hbm, shares_out, freqs_out,
     dosage_ref, shares_ref, freqs_ref, alt_ref, ref_ref,
-    q_slots, f_slots, c_slots, sq_send, sq_recv, sc_send, sc_recv, sf_send, sf_recv,
+    q_slots, f_slots, p_slots, d_slots, c_slots, e_slots,
+    sq_send, sq_recv, sp_send, sp_recv, sc_send, sc_recv, sf_send, sf_recv,
     q_pad, f_pad, qt_ref, qd_ref, qb_ref, fs_ref, fgs_ref,
-    load_sem, q_ss, q_rs, f_ss, f_rs, c_ss, c_rs, sq_ss, sq_rs, sc_ss, sc_rs, sf_ss, sf_rs,
+    load_sem, q_ss, q_rs, f_ss, f_rs, p_ss, p_rs, d_ss, d_rs, c_ss, c_rs,
+    sq_ss, sq_rs, sp_ss, sp_rs, sc_ss, sc_rs, sf_ss, sf_rs,
 ):
     iv, js = lax.axis_index("var"), lax.axis_index("smp")
     pops, ws = shares_ref.shape
@@ -60,8 +71,16 @@
 
     my_mid_chunk = 1 - side
     my_mid = js - middle(my_mid_chunk, 0)
-    is_mid = jnp.logical_and(js >= half - mids, js < half + mids)
+    place = lax.rem(js, half)
+    core, chip, chips = lax.rem(iv, 2), iv // 2, nv // 2
+    owner = 2 * chip + 1
+    is_owner = core == 1
+    central = jnp.logical_and(js >= half - mids, js < half + mids)
+    is_mid = jnp.logical_and(is_owner, central)
+    first = my_mid_chunk * half + 2 * my_mid
     smp_peers = [other_smp(d) for d in range(1, ns)]
+    far_peers = [(1 - side) * (ns - 1 - i) + side * i for i in range(half)]
+    near_peers = [side * half + lax.rem(js + d, half) for d in range(half - 1, 0, -1)]
     var_peers = [lax.rem(iv + d, nv) for d in range(1, nv)]
 
     barrier = pltpu.get_barrier_semaphore()
@@ -81,35 +100,45 @@
     load_q.wait()
     q_own = shares_ref[...]
     q_own = q_own / jnp.sum(q_own, axis=0, keepdims=True)
-    q_slots[0, iv] = q_own
+    q_slots[iv] = q_own
     load_f.wait()
     pl.semaphore_wait(barrier, ns - 1 + nv - 1)
 
-    def smp_copy(src, dst, ss, rs, to):
+    def far_copy(src, dst, ss, rs, smp, var):
         return pltpu.make_async_remote_copy(
-            src_ref=src, dst_ref=dst, send_sem=ss, recv_sem=rs, device_id=(to, iv), device_id_type=mesh_ids)
-
-    def var_copy(src, dst, ss, rs, to):
-        return pltpu.make_async_remote_copy(
-            src_ref=src, dst_ref=dst, send_sem=ss, recv_sem=rs, device_id=(js, to), device_id_type=mesh_ids)
+            src_ref=src, dst_ref=dst, send_sem=ss, recv_sem=rs, device_id=(smp, var), device_id_type=mesh_ids)
 
     def f_copy(to, slot):
-        return smp_copy(f_slots.at[slot], f_slots.at[slot], f_ss.at[to], f_rs.at[slot], to)
-
-    def q_copy(it, to, slot):
-        return var_copy(q_slots.at[it, slot], q_slots.at[it, slot], q_ss.at[it, to], q_rs.at[it, slot], to)
-
-    def sq_copy(it, to, slot):
-        return var_copy(sq_send.at[it, to], sq_recv.at[it, slot], sq_ss.at[it, to], sq_rs.at[it, slot], to)
+        return far_copy(f_slots.at[slot], f_slots.at[slot], f_ss.at[to], f_rs.at[slot], to, iv)
+
+    def e_copy(slot):
+        return far_copy(f_slots.at[first + slot], e_slots.at[slot], d_ss.at[slot], d_rs.at[slot], js, owner)
+
+    def q_copy(to, slot):
+        return far_copy(q_slots.at[slot], q_slots.at[slot], q_ss.at[to], q_rs.at[slot], js, to)
+
+    def sq_copy(to, slot):
+        return far_copy(sq_send.at[to], sq_recv.at[slot], sq_ss.at[to], sq_rs.at[slot], js, to)
 
     def sf_copy(to, slot):
-        return smp_copy(sf_send.at[to], sf_recv.at[slot], sf_ss.at[to], sf_rs.at[slot], to)
-
-    def sc_copy(it, c, i, to, slot):
-        return smp_copy(sc_send.at[it, c, i], sc_recv.at[it, slot], sc_ss.at[it, c, i], sc_rs.at[it, slot], to)
+        return far_copy(sf_send.at[to], sf_recv.at[slot], sf_ss.at[to], sf_rs.at[slot], to, iv)
+
+    def sp_copy(it, j, slot):
+        return far_copy(sp_send.at[it, j], sp_recv.at[it, slot], sp_ss.at[it, j], sp_rs.at[it, slot], js, 2 * j + 1)
+
+    def p_copy(it, to, slot):
+        return far_copy(p_slots.at[it, slot], p_slots.at[it, slot], p_ss.at[it, to], p_rs.at[it, slot], js, to)
+
+    def sc_copy(it, c, i, g, slot):
+        return far_copy(
+            sc_send.at[it, c, i], sc_recv.at[it, g, slot], sc_ss.at[it, c, i], sc_rs.at[it, g, slot],
+            middle(c, i), owner)
 
     def c_copy(it, to, slot):
-        return smp_copy(c_slots.at[it, slot], c_slots.at[it, slot], c_ss.at[it, to], c_rs.at[it, slot], to)
+        return far_copy(c_slots.at[it, slot], c_slots.at[it, slot], c_ss.at[it, 1, to], c_rs.at[it, slot], to, iv)
+
+    def d_copy(it, to, slot):
+        return far_copy(d_slots.at[it], c_slots.at[it, slot], c_ss.at[it, 0, to], c_rs.at[it, slot], to, iv - 1)
 
     sent = []
 
@@ -120,10 +149,10 @@
         else:
             pl.when(when)(copy.start)
 
-    for p in smp_peers:
+    for p in far_peers + near_peers:
         start(f_copy(p, js))
     for p in var_peers:
-        start(q_copy(0, p, iv))
+        start(q_copy(p, iv))
 
     load_d.wait()
     blocks = samples // ROWS
@@ -152,10 +181,16 @@
     for it in range(ITERS):
         last = it + 1 == ITERS
 
-        for p in var_peers:
-            q_copy(it, p, p).wait_recv()
-        for v in range(nv):
-            q_pad[0:pops, v * ws:(v + 1) * ws] = q_slots[it, v]
+        if it == 0:
+            for p in var_peers:
+                q_copy(p, p).wait_recv()
+            for v in range(nv):
+                q_pad[0:pops, v * ws:(v + 1) * ws] = q_slots[v]
+        else:
+            for j in range(chips):
+                pl.when(iv != 2 * j + 1)(p_copy(it, iv, j).wait_recv)
+            for j in range(chips):
+                q_pad[0:pops, 2 * j * ws:2 * (j + 1) * ws] = p_slots[it, j]
         qh, qm = split(q_pad[...], 2)
         qs = jnp.concatenate([qh, qm, qh, qm], axis=0)
         qt_ref[...] = qs.astype(F32).T.astype(BF16)
@@ -171,13 +206,15 @@
                     p = c * half + lax.rem(js + i, half)
                     if t or i:
                         f_copy(p, p).wait_recv()
+                for i in range(2 * t):
+                    start(e_copy(i), jnp.logical_and(central, core == 0))
                 for i in range(half):
                     f_pad[0:pops, i * wf:(i + 1) * wf] = f_slots[c * half + i]
             else:
                 for i in range(mids):
                     slot = c * mids + i
                     copy = c_copy(it, js, slot)
-                    pl.when(middle(c, i) != js)(copy.wait_recv)
+                    pl.when(jnp.logical_or(core == 0, middle(c, i) != js))(copy.wait_recv)
                 for i in range(mids):
                     f_pad[0:pops, i * wc:(i + 1) * wc] = c_slots[it, c * mids + i]
             f_all = f_pad[...]
@@ -190,12 +227,8 @@
             for b in range(blocks):
                 here = slice(b * ROWS, (b + 1) * ROWS)
                 probs = dot(qt_ref[here, :], fs_ref[...])
-                rest = 1.0 - probs
-                inv = 1.0 / (probs * rest)
-                alt = alt_ref[c, here, :] * rest
-                bb = ref_ref[c, here, :] * probs
-                dd = (alt - bb) * inv
-                bb = bb * inv
+                bb = ref_ref[c, here, :] * (1.0 / (1.0 - probs))
+                dd = alt_ref[c, here, :] * (1.0 / probs) - bb
                 dh, bh = dd.astype(BF16), bb.astype(BF16)
                 sums = sums + (dot(qd_ref[:, here], dh) + dot(qb_ref[:, here], bh))
                 kept.append(dh)
@@ -207,70 +240,90 @@
                 for i in range(half):
                     cut = slice(i * wf, (i + 1) * wf)
                     sf_send[c * half + i] = jnp.concatenate([sum_d[:, cut], sum_b[:, cut]], axis=1)
-                for i in range(half):
-                    p = c * half + lax.rem(js + i, half)
-                    if i or t == 0:
-                        start(sf_copy(p, js))
+                for p in far_peers if t == 0 else near_peers:
+                    start(sf_copy(p, js))
             else:
                 stacked = jnp.concatenate([sum_d, sum_b], axis=0)
                 for i in range(mids):
                     sc_send[it, c, i] = stacked[:, i * wc:(i + 1) * wc]
                 for i in range(mids):
-                    to = middle(c, i)
-                    start(sc_copy(it, c, i, to, js), to != js)
+                    start(sc_copy(it, c, i, core, js), jnp.logical_or(core == 0, middle(c, i) != js))
 
         for b in range(blocks):
             sq_acc[b] = sq_acc[b] + dot_nt(fgs_ref[...], kept[b])
         sum_q = jnp.concatenate([x[0:PAD] + x[PAD:2 * PAD] for x in sq_acc], axis=1)
         sum_q = sum_q + (counts - jnp.sum(q_pad[...] * sum_q, axis=0, keepdims=True))
         sum_q = sum_q[0:pops]
-        for v in range(nv):
-            sq_send[it, v] = sum_q[:, v * ws:(v + 1) * ws]
-        for p in var_peers:
-            start(sq_copy(it, p, iv))
-
-        total = sq_send[it, iv]
-        for p in var_peers:
-            sq_copy(it, p, p).wait_recv()
-            total = total + sq_recv[it, p]
-        numer = q_own * total
-        q_own = (numer + 0.5) / (jnp.sum(numer, axis=0, keepdims=True) + 0.5 * pops)
-        if last:
-            shares_out[...] = q_own
+        if not last:
+            for j in range(chips):
+                sp_send[it, j] = sum_q[:, 2 * j * ws:2 * (j + 1) * ws]
+            for j in range(chips):
+                start(sp_copy(it, j, iv), iv != 2 * j + 1)
+
+            @pl.when(is_owner)
+            def _():
+                total = sp_send[it, chip]
+                for p in var_peers:
+                    sp_copy(it, chip, p).wait_recv()
+                    total = total + sp_recv[it, p]
+                if it == 0:
+                    q_old = jnp.concatenate([q_slots[2 * chip], q_slots[2 * chip + 1]], axis=1)
+                else:
+                    q_old = p_slots[it, chip]
+                p_slots[it + 1, chip] = renewed_shares(q_old, total)
+
+            for p in var_peers:
+                start(p_copy(it + 1, p, chip), is_owner)
+
+            slot = my_mid_chunk * mids + my_mid
+            for g in (1, 0):
+
+                @pl.when(is_mid)
+                def _():
+                    if g:
+                        total = sc_send[it, my_mid_chunk, my_mid]
+                        peers = smp_peers
+                    else:
+                        total = jnp.zeros((2 * pops, wc), F32)
+                        peers = smp_peers + [js]
+                    for p in peers:
+                        sc_copy(it, my_mid_chunk, my_mid, g, p).wait_recv()
+                        total = total + sc_recv[it, g, p]
+                    if it == 0 and g:
+                        f_old = jnp.concatenate([f_slots[first], f_slots[first + 1]], axis=1)
+                    elif it == 0:
+                        e_copy(0).wait_recv()
+                        e_copy(1).wait_recv()
+                        f_old = jnp.concatenate([e_slots[0], e_slots[1]], axis=1)
+                    else:
+                        f_old = c_slots[it, slot] if g else d_slots[it]
+                    new = renewed_freqs(f_old, total[0:pops], total[pops:2 * pops])
+                    if g:
+                        c_slots[it + 1, slot] = new
+                    else:
+                        d_slots[it + 1] = new
+
+                for p in far_peers + near_peers + ([] if g else [js]):
+                    start((c_copy if g else d_copy)(it + 1, p, slot), is_mid)
         else:
-            q_slots[it + 1, iv] = q_own
+            for v in range(nv):
+                sq_send[v] = sum_q[:, v * ws:(v + 1) * ws]
             for p in var_peers:
-                start(q_copy(it + 1, p, iv))
-
-        if last:
-            place = lax.rem(js, half)
+                start(sq_copy(p, iv))
+            total = sq_send[iv]
+            for p in var_peers:
+                sq_copy(p, p).wait_recv()
+                total = total + sq_recv[p]
+            pair = p_slots[it, chip]
+            shares_out[...] = renewed_shares(jnp.where(core == 0, pair[:, 0:ws], pair[:, ws:2 * ws]), total)
+
             pair = c_slots[it, side * mids + place // 2]
             f_own = jnp.where(lax.rem(place, 2) == 0, pair[:, 0:wf], pair[:, wf:2 * wf])
             total = sf_send[js]
             for p in smp_peers:
                 sf_copy(p, p).wait_recv()
                 total = total + sf_recv[p]
-            sum_d, sum_b = total[:, 0:wf], total[:, wf:2 * wf]
-            freqs_out[...] = (f_own * (sum_d + sum_b) + 0.5) / (f_own * sum_d + sum_b + 1.0)
-        else:
-            slot = my_mid_chunk * mids + my_mid
-
-            @pl.when(is_mid)
-            def _():
-                total = sc_send[it, my_mid_chunk, my_mid]
-                for p in smp_peers:
-                    sc_copy(it, my_mid_chunk, my_mid, js, p).wait_recv()
-                    total = total + sc_recv[it, p]
-                if it == 0:
-                    first = my_mid_chunk * half + 2 * my_mid
-                    f_old = jnp.concatenate([f_slots[first], f_slots[first + 1]], axis=1)
-                else:
-                    f_old = c_slots[it, slot]
-                sum_d, sum_b = total[0:pops], total[pops:2 * pops]
-                c_slots[it + 1, slot] = (f_old * (sum_d + sum_b) + 0.5) / (f_old * sum_d + sum_b + 1.0)
-
-            for p in smp_peers:
-                start(c_copy(it + 1, p, slot), is_mid)
+            freqs_out[...] = renewed_freqs(f_own, total[:, 0:wf], total[:, wf:2 * wf])
 
     for copy, when in sent:
         if when is None:
@@ -291,6 +344,7 @@
     samples = words * CODES
     chunk = variants // 2
     mids = ns // 4
+    chips = nv // 2
     wc = chunk // mids
     vmem = pl.BlockSpec(memory_space=pltpu.VMEM)
     hbm = pl.BlockSpec(memory_space=pl.ANY)
@@ -307,13 +361,18 @@
             pltpu.VMEM((pops, wf), F32),
             pltpu.VMEM((2, samples, chunk), F32),
             pltpu.VMEM((2, samples, chunk), F32),
-            pltpu.VMEM((ITERS, nv, pops, ws), F32),
+            pltpu.VMEM((nv, pops, ws), F32),
             pltpu.VMEM((ns, pops, wf), F32),
+            pltpu.VMEM((ITERS, chips, pops, 2 * ws), F32),
+            pltpu.VMEM((ITERS, pops, wc), F32),
             pltpu.VMEM((ITERS, 2 * mids, pops, wc), F32),
-            pltpu.VMEM((ITERS, nv, pops, ws), F32),
-            pltpu.VMEM((ITERS, nv, pops, ws), F32),
+            pltpu.VMEM((2, pops, wf), F32),
+            pltpu.VMEM((nv, pops, ws), F32),
+            pltpu.VMEM((nv, pops, ws), F32),
+            pltpu.VMEM((ITERS, chips, pops, 2 * ws), F32),
+            pltpu.VMEM((ITERS, nv, pops, 2 * ws), F32),
             pltpu.VMEM((ITERS, 2, mids, 2 * pops, wc), F32),
-            pltpu.VMEM((ITERS, ns, 2 * pops, wc), F32),
+            pltpu.VMEM((ITERS, 2, ns, 2 * pops, wc), F32),
             pltpu.VMEM((ns, pops, 2 * wf), F32),
             pltpu.VMEM((ns, pops, 2 * wf), F32),
             pltpu.VMEM((PAD, samples), F32),
@@ -324,11 +383,14 @@
             pltpu.VMEM((4 * PAD, chunk), BF16),
             pltpu.VMEM((2 * PAD, chunk), BF16),
             dma((3,)),
-            dma((ITERS, nv)), dma((ITERS, nv)),
+            dma((nv,)), dma((nv,)),
             dma((ns,)), dma((ns,)),
-            dma((ITERS, ns)), dma((ITERS, 2 * mids)),
-            dma((ITERS, nv)), dma((ITERS, nv)),
-            dma((ITERS, 2, mids)), dma((ITERS, ns)),
+            dma((ITERS, nv)), dma((ITERS, chips)),
+            dma((2,)), dma((2,)),
+            dma((ITERS, 2, ns)), dma((ITERS, 2 * mids)),
+            dma((nv,)), dma((nv,)),
+            dma((ITERS, chips)), dma((ITERS, nv)),
+            dma((ITERS, 2, mids)), dma((ITERS, 2, ns)),
             dma((ns,)), dma((ns,)),
         ],
         compiler_params=pltpu.CompilerParams(collective_id=0, has_side_effects=True),

time: 25 us -> 24.4 us (0.976)
  Pallas kernels: 24.2 us -> 23.6 us
    pallas_call x1, Pallas kernels: 23.6 us -> 22.9 us  [body(): pl.pallas_call(functools.partial(em_kernel, nv, ns), out_shape=(pltpu.VME...]
where the time goes in v4:
time: 24.4 us; the launch traced here: 24.2 us
  Pallas kernels  23.6 us (97%)
  between operations  0.64 us (3%)
    pallas_call x1, Pallas kernels, body(): pl.pallas_call(functools.partial(em_kernel, nv, ns), out_shape=(pltpu.VME...  22.9 us
    pallas_call x1, Pallas kernels, body(): pl.pallas_call(hand_out, out_shape=shapes, in_specs=[vmem, vmem], out_spe...  0.61 us

profile of v4, /device:TPU:0, one launch (start us, length us, event | category | flops | bytes accessed | tf_op | source)
XLA Modules:
  0.0 24.2 jit_solution(3546140392579132441)
XLA Ops:
  0.6 22.9 %shard_map.50 = (f32[12,256]{1,0:T(8,128)S(1)}, f32[12,64]{1,0:T(8,128)S(1)}) custom-call(s32[64,512]{1,0:T(8,128)} %dosage_hbm.1, f32[12,256]{1,0:T(8,128)} %shares_hbm.1, f32[12,64]{1,0:T(8,128)} %freqs_hbm.1), custom_call_target="tpu_custom_call" | custom-call | flops 200000000 | bytes 400000 | tf_op jit(solution)/shard_map/pallas_call | solution.py:353
  23.6 0.6 %shard_map.51 = (f32[12,256]{1,0:T(8,128)}, f32[12,64]{1,0:T(8,128)}) custom-call(f32[12,256]{1,0:T(8,128)S(1)} %get-tuple-element.4.shares_ref, f32[12,64]{1,0:T(8,128)S(1)} %get-tuple-element.5.freqs_ref), custom_call_target="tpu_custom_call" | custom-call | tf_op jit(solution)/shard_map/pallas_call | solution.py:401

commit v5 on v4

--- a/solution.py
+++ b/solution.py
@@ -42,12 +42,16 @@
     return (old * (sum_d + sum_b) + 0.5) / (old * sum_d + sum_b + 1.0)
 
 
+def full_rows(x):
+    return jnp.concatenate([x, jnp.zeros((PAD - x.shape[0], x.shape[1]), x.dtype)], axis=0)
+
+
 def em_kernel(
     nv, ns, dosage_hbm, shares_hbm, freqs_hbm, shares_out, freqs_out,
-    dosage_ref, shares_ref, freqs_ref, alt_ref, ref_ref,
+    dosage_ref, shares_ref, freqs_ref, w_ref,
     q_slots, f_slots, p_slots, d_slots, c_slots, e_slots,
-    sq_send, sq_recv, sp_send, sp_recv, sc_send, sc_recv, sf_send, sf_recv,
-    q_pad, f_pad, qt_ref, qd_ref, qb_ref, fs_ref, fgs_ref,
+    sq_send, sq_recv, sp_send, sp_recv, sc_send, sc_recv, sf_recv,
+    q_pad, qt_ref, qd_ref, qb_ref, sq_ref,
     load_sem, q_ss, q_rs, f_ss, f_rs, p_ss, p_rs, d_ss, d_rs, c_ss, c_rs,
     sq_ss, sq_rs, sp_ss, sp_rs, sc_ss, sc_rs, sf_ss, sf_rs,
 ):
@@ -84,24 +88,28 @@
     var_peers = [lax.rem(iv + d, nv) for d in range(1, nv)]
 
     barrier = pltpu.get_barrier_semaphore()
-    for p in smp_peers:
+    for p in far_peers + near_peers:
         pl.semaphore_signal(barrier, inc=1, device_id=(p, iv), device_id_type=mesh_ids)
     for p in var_peers:
         pl.semaphore_signal(barrier, inc=1, device_id=(js, p), device_id_type=mesh_ids)
 
     load_q = pltpu.make_async_copy(shares_hbm, shares_ref, load_sem.at[0])
-    load_f = pltpu.make_async_copy(freqs_hbm, f_slots.at[js], load_sem.at[1])
+    load_f = pltpu.make_async_copy(freqs_hbm, freqs_ref, load_sem.at[1])
     load_d = pltpu.make_async_copy(dosage_hbm, dosage_ref, load_sem.at[2])
     load_q.start()
     load_f.start()
     load_d.start()
     q_pad[...] = jnp.zeros_like(q_pad)
-    f_pad[...] = jnp.zeros_like(f_pad)
     load_q.wait()
     q_own = shares_ref[...]
     q_own = q_own / jnp.sum(q_own, axis=0, keepdims=True)
     q_slots[iv] = q_own
     load_f.wait()
+    f_own = freqs_ref[...]
+    beside = jnp.zeros_like(f_own)
+    odd = lax.rem(js, 2) == 1
+    f_own = jnp.where(odd, jnp.concatenate([beside, f_own], axis=1), jnp.concatenate([f_own, beside], axis=1))
+    f_slots[js] = full_rows(f_own)
     pl.semaphore_wait(barrier, ns - 1 + nv - 1)
 
     def far_copy(src, dst, ss, rs, smp, var):
@@ -120,8 +128,9 @@
     def sq_copy(to, slot):
         return far_copy(sq_send.at[to], sq_recv.at[slot], sq_ss.at[to], sq_rs.at[slot], js, to)
 
-    def sf_copy(to, slot):
-        return far_copy(sf_send.at[to], sf_recv.at[slot], sf_ss.at[to], sf_rs.at[slot], to, iv)
+    def sf_copy(c, to, slot):
+        return far_copy(
+            sc_send.at[ITERS - 1, c, lax.rem(to, half) // 2], sf_recv.at[slot], sf_ss.at[to], sf_rs.at[slot], to, iv)
 
     def sp_copy(it, j, slot):
         return far_copy(sp_send.at[it, j], sp_recv.at[it, slot], sp_ss.at[it, j], sp_rs.at[it, slot], js, 2 * j + 1)
@@ -172,8 +181,8 @@
             live = codes < 3
             alt = jnp.where(live, codes.astype(F32), 0.0)
             both = jnp.where(live, 2.0, 0.0)
-            alt_ref[c, here, :] = (alt * step).reshape(ROWS, chunk)
-            ref_ref[c, here, :] = ((both - alt) * step).reshape(ROWS, chunk)
+            w_ref[c, here, 0:chunk] = (alt * step).reshape(ROWS, chunk)
+            w_ref[c, here, chunk:2 * chunk] = ((both - alt) * step).reshape(ROWS, chunk)
             count = count + dot_nt(ones, both.reshape(ROWS, chunk).astype(BF16))
         counts.append(count[0:1])
     counts = jnp.concatenate(counts, axis=1)
@@ -194,11 +203,11 @@
         qh, qm = split(q_pad[...], 2)
         qs = jnp.concatenate([qh, qm, qh, qm], axis=0)
         qt_ref[...] = qs.astype(F32).T.astype(BF16)
+        qh, qm = qh.astype(F32)[0:pops], qm.astype(F32)[0:pops]
         none = jnp.zeros_like(qh)
-        qd_ref[...] = jnp.concatenate([qh, none, qm, none], axis=0)
-        qb_ref[...] = jnp.concatenate([none, qh, none, qm], axis=0)
-
-        sq_acc = [jnp.zeros((2 * PAD, ROWS), F32) for _ in range(blocks)]
+        qd_ref[...] = jnp.concatenate([qh, none, qm, none], axis=0).astype(BF16)
+        qb_ref[...] = jnp.concatenate([none, qh, none, qm], axis=0).astype(BF16)
+
         for t in range(2):
             c = side if (it == 0) == (t == 0) else 1 - side
             if it == 0:
@@ -208,50 +217,41 @@
                         f_copy(p, p).wait_recv()
                 for i in range(2 * t):
                     start(e_copy(i), jnp.logical_and(central, core == 0))
-                for i in range(half):
-                    f_pad[0:pops, i * wf:(i + 1) * wf] = f_slots[c * half + i]
+                f_all = [f_slots[c * half + 2 * i] + f_slots[c * half + 2 * i + 1] for i in range(mids)]
             else:
                 for i in range(mids):
                     slot = c * mids + i
                     copy = c_copy(it, js, slot)
                     pl.when(jnp.logical_or(core == 0, middle(c, i) != js))(copy.wait_recv)
-                for i in range(mids):
-                    f_pad[0:pops, i * wc:(i + 1) * wc] = c_slots[it, c * mids + i]
-            f_all = f_pad[...]
-            fh, fm = split(f_all, 2)
-            fs_ref[...] = jnp.concatenate([fh, fh, fm, fm], axis=0)
-            fgs_ref[...] = jnp.concatenate([fh, fm], axis=0)
+                f_all = [c_slots[it, c * mids + i] for i in range(mids)]
+            fh, fm = split(jnp.concatenate(f_all, axis=1), 2)
+            fs = jnp.concatenate([fh, fh, fm, fm], axis=0)
+            fg = jnp.concatenate([fh, fm], axis=0)
 
             kept = []
-            sums = jnp.zeros((4 * PAD, chunk), F32)
+            sums = jnp.zeros((4 * pops, chunk), F32)
             for b in range(blocks):
                 here = slice(b * ROWS, (b + 1) * ROWS)
-                probs = dot(qt_ref[here, :], fs_ref[...])
-                bb = ref_ref[c, here, :] * (1.0 / (1.0 - probs))
-                dd = alt_ref[c, here, :] * (1.0 / probs) - bb
+                probs = dot(qt_ref[here, :], fs)
+                bb = w_ref[c, here, chunk:2 * chunk] * (1.0 / (1.0 - probs))
+                dd = w_ref[c, here, 0:chunk] * (1.0 / probs) - bb
                 dh, bh = dd.astype(BF16), bb.astype(BF16)
                 sums = sums + (dot(qd_ref[:, here], dh) + dot(qb_ref[:, here], bh))
                 kept.append(dh)
-                if t == 0:
-                    sq_acc[b] = sq_acc[b] + dot_nt(fgs_ref[...], kept[b])
-            sums = sums[0:2 * PAD] + sums[2 * PAD:4 * PAD]
-            sum_d, sum_b = sums[0:pops], sums[PAD:PAD + pops]
+            sums = sums[0:2 * pops] + sums[2 * pops:4 * pops]
+            for i in range(mids):
+                sc_send[it, c, i] = sums[:, i * wc:(i + 1) * wc]
             if last:
-                for i in range(half):
-                    cut = slice(i * wf, (i + 1) * wf)
-                    sf_send[c * half + i] = jnp.concatenate([sum_d[:, cut], sum_b[:, cut]], axis=1)
                 for p in far_peers if t == 0 else near_peers:
-                    start(sf_copy(p, js))
+                    start(sf_copy(c, p, js))
             else:
-                stacked = jnp.concatenate([sum_d, sum_b], axis=0)
-                for i in range(mids):
-                    sc_send[it, c, i] = stacked[:, i * wc:(i + 1) * wc]
                 for i in range(mids):
                     start(sc_copy(it, c, i, core, js), jnp.logical_or(core == 0, middle(c, i) != js))
-
-        for b in range(blocks):
-            sq_acc[b] = sq_acc[b] + dot_nt(fgs_ref[...], kept[b])
-        sum_q = jnp.concatenate([x[0:PAD] + x[PAD:2 * PAD] for x in sq_acc], axis=1)
+            if t == 0:
+                sq_ref[...] = jnp.concatenate([dot_nt(fg, x) for x in kept], axis=1)
+
+        sum_q = sq_ref[...] + jnp.concatenate([dot_nt(fg, x) for x in kept], axis=1)
+        sum_q = sum_q[0:PAD] + sum_q[PAD:2 * PAD]
         sum_q = sum_q + (counts - jnp.sum(q_pad[...] * sum_q, axis=0, keepdims=True))
         sum_q = sum_q[0:pops]
         if not last:
@@ -290,14 +290,14 @@
                         sc_copy(it, my_mid_chunk, my_mid, g, p).wait_recv()
                         total = total + sc_recv[it, g, p]
                     if it == 0 and g:
-                        f_old = jnp.concatenate([f_slots[first], f_slots[first + 1]], axis=1)
+                        f_old = f_slots[first] + f_slots[first + 1]
                     elif it == 0:
                         e_copy(0).wait_recv()
                         e_copy(1).wait_recv()
-                        f_old = jnp.concatenate([e_slots[0], e_slots[1]], axis=1)
+                        f_old = e_slots[0] + e_slots[1]
                     else:
                         f_old = c_slots[it, slot] if g else d_slots[it]
-                    new = renewed_freqs(f_old, total[0:pops], total[pops:2 * pops])
+                    new = full_rows(renewed_freqs(f_old[0:pops], total[0:pops], total[pops:2 * pops]))
                     if g:
                         c_slots[it + 1, slot] = new
                     else:
@@ -317,13 +317,12 @@
             pair = p_slots[it, chip]
             shares_out[...] = renewed_shares(jnp.where(core == 0, pair[:, 0:ws], pair[:, ws:2 * ws]), total)
 
-            pair = c_slots[it, side * mids + place // 2]
-            f_own = jnp.where(lax.rem(place, 2) == 0, pair[:, 0:wf], pair[:, wf:2 * wf])
-            total = sf_send[js]
+            total = sc_send[it, side, place // 2]
             for p in smp_peers:
-                sf_copy(p, p).wait_recv()
+                sf_copy(side, p, p).wait_recv()
                 total = total + sf_recv[p]
-            freqs_out[...] = renewed_freqs(f_own, total[:, 0:wf], total[:, wf:2 * wf])
+            pair = renewed_freqs(c_slots[it, side * mids + place // 2][0:pops], total[0:pops], total[pops:2 * pops])
+            freqs_out[...] = jnp.where(odd, pair[:, wf:2 * wf], pair[:, 0:wf])
 
     for copy, when in sent:
         if when is None:
@@ -332,9 +331,15 @@
             pl.when(when)(copy.wait_send)
 
 
-def hand_out(shares_ref, freqs_ref, shares_out, freqs_out):
-    shares_out[...] = shares_ref[...]
-    freqs_out[...] = freqs_ref[...]
+def hand_out(shares_ref, freqs_ref, shares_out, freqs_out, sems):
+    copies = [
+        pltpu.make_async_copy(shares_ref, shares_out, sems.at[0]),
+        pltpu.make_async_copy(freqs_ref, freqs_out, sems.at[1]),
+    ]
+    for copy in copies:
+        copy.start()
+    for copy in copies:
+        copy.wait()
 
 
 def body(nv, ns, dosage, shares_init, freqs_init):
@@ -359,29 +364,25 @@
             pltpu.VMEM((words, variants), jnp.int32),
             pltpu.VMEM((pops, ws), F32),
             pltpu.VMEM((pops, wf), F32),
-            pltpu.VMEM((2, samples, chunk), F32),
-            pltpu.VMEM((2, samples, chunk), F32),
+            pltpu.VMEM((2, samples, 2 * chunk), F32),
             pltpu.VMEM((nv, pops, ws), F32),
-            pltpu.VMEM((ns, pops, wf), F32),
+            pltpu.VMEM((ns, PAD, wc), F32),
             pltpu.VMEM((ITERS, chips, pops, 2 * ws), F32),
-            pltpu.VMEM((ITERS, pops, wc), F32),
-            pltpu.VMEM((ITERS, 2 * mids, pops, wc), F32),
-            pltpu.VMEM((2, pops, wf), F32),
+            pltpu.VMEM((ITERS, PAD, wc), F32),
+            pltpu.VMEM((ITERS, 2 * mids, PAD, wc), F32),
+            pltpu.VMEM((2, PAD, wc), F32),
             pltpu.VMEM((nv, pops, ws), F32),
             pltpu.VMEM((nv, pops, ws), F32),
             pltpu.VMEM((ITERS, chips, pops, 2 * ws), F32),
             pltpu.VMEM((ITERS, nv, pops, 2 * ws), F32),
             pltpu.VMEM((ITERS, 2, mids, 2 * pops, wc), F32),
             pltpu.VMEM((ITERS, 2, ns, 2 * pops, wc), F32),
-            pltpu.VMEM((ns, pops, 2 * wf), F32),
-            pltpu.VMEM((ns, pops, 2 * wf), F32),
+            pltpu.VMEM((ns, 2 * pops, wc), F32),
             pltpu.VMEM((PAD, samples), F32),
-            pltpu.VMEM((PAD, chunk), F32),
             pltpu.VMEM((samples, 4 * PAD), BF16),
-            pltpu.VMEM((4 * PAD, samples), BF16),
-            pltpu.VMEM((4 * PAD, samples), BF16),
-            pltpu.VMEM((4 * PAD, chunk), BF16),
-            pltpu.VMEM((2 * PAD, chunk), BF16),
+            pltpu.VMEM((4 * pops, samples), BF16),
+            pltpu.VMEM((4 * pops, samples), BF16),
+            pltpu.VMEM((2 * PAD, samples), F32),
             dma((3,)),
             dma((nv,)), dma((nv,)),
             dma((ns,)), dma((ns,)),
@@ -399,7 +400,7 @@
     shares = pltpu.with_memory_space_constraint(shares, pltpu.VMEM)
     freqs = pltpu.with_memory_space_constraint(freqs, pltpu.VMEM)
     return pl.pallas_call(
-        hand_out, out_shape=shapes, in_specs=[vmem, vmem], out_specs=(vmem, vmem),
+        hand_out, out_shape=shapes, in_specs=[vmem, vmem], out_specs=(hbm, hbm), scratch_shapes=[dma((2,))],
     )(shares, freqs)
 
 

time: 24.4 us -> 24.4 us (level)
  no operation moved by 1% of the time
where the time goes in v5:
time: 24.4 us; the launch traced here: 24.2 us
  Pallas kernels  23.5 us (96%)
  between operations  0.64 us (3%)
    pallas_call x1, Pallas kernels, body(): pl.pallas_call(functools.partial(em_kernel, nv, ns), out_shape=(pltpu.VME...  22.9 us
    pallas_call x1, Pallas kernels, body(): pl.pallas_call(hand_out, out_shape=shapes, in_specs=[vmem, vmem], out_spe...  0.63 us

profile of v5, /device:TPU:0, one launch (start us, length us, event | category | flops | bytes accessed | tf_op | source)
XLA Modules:
  0.0 24.2 jit_solution(1624100569476163776)
XLA Ops:
  0.6 22.9 %shard_map.50 = (f32[12,256]{1,0:T(8,128)S(1)}, f32[12,64]{1,0:T(8,128)S(1)}) custom-call(s32[64,512]{1,0:T(8,128)} %dosage_hbm.1, f32[12,256]{1,0:T(8,128)} %shares_hbm.1, f32[12,64]{1,0:T(8,128)} %freqs_hbm.1), custom_call_target="tpu_custom_call" | custom-call | flops 200000000 | bytes 400000 | tf_op jit(solution)/shard_map/pallas_call | solution.py:358
  23.5 0.6 %shard_map.51 = (f32[12,256]{1,0:T(8,128)}, f32[12,64]{1,0:T(8,128)}) custom-call(f32[12,256]{1,0:T(8,128)S(1)} %get-tuple-element.4.shares_ref, f32[12,64]{1,0:T(8,128)S(1)} %get-tuple-element.5.freqs_ref), custom_call_target="tpu_custom_call" | custom-call | tf_op jit(solution)/shard_map/pallas_call | solution.py:402

commit v6 on v5

--- a/solution.py
+++ b/solution.py
@@ -317,18 +317,18 @@
             pair = p_slots[it, chip]
             shares_out[...] = renewed_shares(jnp.where(core == 0, pair[:, 0:ws], pair[:, ws:2 * ws]), total)
 
+            for copy, when in sent:
+                if when is None:
+                    copy.wait_send()
+                else:
+                    pl.when(when)(copy.wait_send)
+
             total = sc_send[it, side, place // 2]
             for p in smp_peers:
                 sf_copy(side, p, p).wait_recv()
                 total = total + sf_recv[p]
             pair = renewed_freqs(c_slots[it, side * mids + place // 2][0:pops], total[0:pops], total[pops:2 * pops])
             freqs_out[...] = jnp.where(odd, pair[:, wf:2 * wf], pair[:, 0:wf])
-
-    for copy, when in sent:
-        if when is None:
-            copy.wait_send()
-        else:
-            pl.when(when)(copy.wait_send)
 
 
 def hand_out(shares_ref, freqs_ref, shares_out, freqs_out, sems):

time: 24.4 us -> 24.3 us (level)
  no operation moved by 1% of the time
where the time goes in v6:
time: 24.3 us; the launch traced here: 24.1 us
  Pallas kernels  23.5 us (97%)
  between operations  0.64 us (3%)
    pallas_call x1, Pallas kernels, body(): pl.pallas_call(functools.partial(em_kernel, nv, ns), out_shape=(pltpu.VME...  22.8 us
    pallas_call x1, Pallas kernels, body(): pl.pallas_call(hand_out, out_shape=shapes, in_specs=[vmem, vmem], out_spe...  0.63 us

profile of v6, /device:TPU:0, one launch (start us, length us, event | category | flops | bytes accessed | tf_op | source)
XLA Modules:
  0.0 24.1 jit_solution(8308475159417748744)
XLA Ops:
  0.6 22.8 %shard_map.50 = (f32[12,256]{1,0:T(8,128)S(1)}, f32[12,64]{1,0:T(8,128)S(1)}) custom-call(s32[64,512]{1,0:T(8,128)} %dosage_hbm.1, f32[12,256]{1,0:T(8,128)} %shares_hbm.1, f32[12,64]{1,0:T(8,128)} %freqs_hbm.1), custom_call_target="tpu_custom_call" | custom-call | flops 200000000 | bytes 400000 | tf_op jit(solution)/shard_map/pallas_call | solution.py:358
  23.5 0.6 %shard_map.51 = (f32[12,256]{1,0:T(8,128)}, f32[12,64]{1,0:T(8,128)}) custom-call(f32[12,256]{1,0:T(8,128)S(1)} %get-tuple-element.4.shares_ref, f32[12,64]{1,0:T(8,128)S(1)} %get-tuple-element.5.freqs_ref), custom_call_target="tpu_custom_call" | custom-call | tf_op jit(solution)/shard_map/pallas_call | solution.py:402

commit v7 on v6

--- a/solution.py
+++ b/solution.py
@@ -10,7 +10,7 @@
 ITERS = 2
 CODES = 16
 PAD = 16
-ROWS = 512
+ROWS = 128
 LEVELS = 64
 F32 = jnp.float32
 BF16 = jnp.bfloat16

time: 24.3 us -> 24.1 us (level)
  Pallas kernels: 23.5 us -> 23.2 us
    pallas_call x1, Pallas kernels: 22.8 us -> 22.6 us  [body(): pl.pallas_call(functools.partial(em_kernel, nv, ns), out_shape=(pltpu.VME...]
where the time goes in v7:
time: 24.1 us; the launch traced here: 23.8 us
  Pallas kernels  23.2 us (96%)
  between operations  0.64 us (3%)
    pallas_call x1, Pallas kernels, body(): pl.pallas_call(functools.partial(em_kernel, nv, ns), out_shape=(pltpu.VME...  22.6 us
    pallas_call x1, Pallas kernels, body(): pl.pallas_call(hand_out, out_shape=shapes, in_specs=[vmem, vmem], out_spe...  0.63 us

profile of v7, /device:TPU:0, one launch (start us, length us, event | category | flops | bytes accessed | tf_op | source)
XLA Modules:
  0.0 23.8 jit_solution(4467419588947381052)
XLA Ops:
  0.6 22.6 %shard_map.50 = (f32[12,256]{1,0:T(8,128)S(1)}, f32[12,64]{1,0:T(8,128)S(1)}) custom-call(s32[64,512]{1,0:T(8,128)} %dosage_hbm.1, f32[12,256]{1,0:T(8,128)} %shares_hbm.1, f32[12,64]{1,0:T(8,128)} %freqs_hbm.1), custom_call_target="tpu_custom_call" | custom-call | flops 200000000 | bytes 400000 | tf_op jit(solution)/shard_map/pallas_call | solution.py:358
  23.2 0.6 %shard_map.51 = (f32[12,256]{1,0:T(8,128)}, f32[12,64]{1,0:T(8,128)}) custom-call(f32[12,256]{1,0:T(8,128)S(1)} %get-tuple-element.4.shares_ref, f32[12,64]{1,0:T(8,128)S(1)} %get-tuple-element.5.freqs_ref), custom_call_target="tpu_custom_call" | custom-call | tf_op jit(solution)/shard_map/pallas_call | solution.py:402

commit v8 on v7

--- a/solution.py
+++ b/solution.py
@@ -158,10 +158,12 @@
         else:
             pl.when(when)(copy.start)
 
-    for p in far_peers + near_peers:
+    for p in far_peers:
         start(f_copy(p, js))
     for p in var_peers:
         start(q_copy(p, iv))
+    for p in near_peers:
+        start(f_copy(p, js))
 
     load_d.wait()
     blocks = samples // ROWS
@@ -248,9 +250,9 @@
                 for i in range(mids):
                     start(sc_copy(it, c, i, core, js), jnp.logical_or(core == 0, middle(c, i) != js))
             if t == 0:
-                sq_ref[...] = jnp.concatenate([dot_nt(fg, x) for x in kept], axis=1)
-
-        sum_q = sq_ref[...] + jnp.concatenate([dot_nt(fg, x) for x in kept], axis=1)
+                sq_ref[...] = dot_nt(fg, jnp.concatenate(kept, axis=0))
+
+        sum_q = sq_ref[...] + dot_nt(fg, jnp.concatenate(kept, axis=0))
         sum_q = sum_q[0:PAD] + sum_q[PAD:2 * PAD]
         sum_q = sum_q + (counts - jnp.sum(q_pad[...] * sum_q, axis=0, keepdims=True))
         sum_q = sum_q[0:pops]

time: 24.1 us -> 24.2 us (level)
  no operation moved by 1% of the time
where the time goes in v8:
time: 24.2 us; the launch traced here: 23.9 us
  Pallas kernels  23.3 us (96%)
  between operations  0.64 us (3%)
    pallas_call x1, Pallas kernels, body(): pl.pallas_call(functools.partial(em_kernel, nv, ns), out_shape=(pltpu.VME...  22.7 us
    pallas_call x1, Pallas kernels, body(): pl.pallas_call(hand_out, out_shape=shapes, in_specs=[vmem, vmem], out_spe...  0.63 us

profile of v8, /device:TPU:0, one launch (start us, length us, event | category | flops | bytes accessed | tf_op | source)
XLA Modules:
  0.0 23.9 jit_solution(11835799727939206422)
XLA Ops:
  0.6 22.7 %shard_map.50 = (f32[12,256]{1,0:T(8,128)S(1)}, f32[12,64]{1,0:T(8,128)S(1)}) custom-call(s32[64,512]{1,0:T(8,128)} %dosage_hbm.1, f32[12,256]{1,0:T(8,128)} %shares_hbm.1, f32[12,64]{1,0:T(8,128)} %freqs_hbm.1), custom_call_target="tpu_custom_call" | custom-call | flops 200000000 | bytes 400000 | tf_op jit(solution)/shard_map/pallas_call | solution.py:360
  23.3 0.6 %shard_map.51 = (f32[12,256]{1,0:T(8,128)}, f32[12,64]{1,0:T(8,128)}) custom-call(f32[12,256]{1,0:T(8,128)S(1)} %get-tuple-element.4.shares_ref, f32[12,64]{1,0:T(8,128)S(1)} %get-tuple-element.5.freqs_ref), custom_call_target="tpu_custom_call" | custom-call | tf_op jit(solution)/shard_map/pallas_call | solution.py:404
